TPU v7x, 32 devices: a whole 2x2x4 slice. The times are simulated.
32 devices in a mesh: grp: 2 (over x), rep: 4 (over z), tp: 4 (over y, core).
Axes of the slice: x: 2, y: 2, z: 4, core: 2. Of those that a mesh axis runs over, the one named last changes fastest.
Arguments:
- grad_parts: float32 [4, 5120, 2048], P('tp', ('grp', 'rep')), may hold values from -124 to 124
- master: float32 [5120, 2048], P(('grp', 'rep'), 'tp'), may hold values from -0.078125 to 0.078125
- moment_one: float32 [5120, 2048], P(('grp', 'rep'), 'tp'), may hold values from -1.5 to 1.5
- moment_two: float32 [5120, 2048], P(('grp', 'rep'), 'tp'), may hold values from 0.003 to 0.03
- hidden_in: bfloat16 [32, 4, 5120], P(('grp', 'rep')), may hold values from -6 to 6
- queries: bfloat16 [32, 4, 5120], P(('grp', 'rep'), None, 'tp'), may hold values from -8 to 8
- cache_keys: bfloat16 [32, 1024, 1024], P(('grp', 'rep'), None, 'tp'), may hold values from -8 to 8
- cache_values: bfloat16 [32, 1024, 1024], P(('grp', 'rep'), None, 'tp'), may hold values from -6 to 6
- cache_lengths: int32 [32], P(('grp', 'rep')), may hold values from 16 to 1024
Outputs:
- new_moment_one: float32 [5120, 2048], P(('grp', 'rep'), 'tp')
- new_moment_two: float32 [5120, 2048], P(('grp', 'rep'), 'tp')
- new_entries: bfloat16 [32, 4, 2048], P(('grp', 'rep'), None, 'tp')
- attended: bfloat16 [32, 4, 5120], P(('grp', 'rep'), None, 'tp')
Inputs may be any that keep to these rules, and one draw needn't show every extreme that they name: `cache_lengths`: cache slots at or after a row's length hold no part of its cache.
All inputs are finite; a program needn't handle non-finite values.
Results may differ from a plain program's by a relative error of at most 0.0051.
Values may be sent and summed in bfloat16 or wider, within the bound.
A program may use at most 64 MiB of HBM per device.

v0:
```python
import math

import jax
import jax.numpy as jnp
from jax import lax
from jax.sharding import PartitionSpec as P

D = 5120
QH = 40
KVH = 8
HD = 128


BETA_ONE = 0.9
BETA_TWO = 0.999
FIRST_CORR = 0.9999734386011124
SECOND_CORR = 0.09520785288629041
LEARN_RATE = 0.003
EPSILON = 1e-08
ROPE_BASE = 1000000.0
NEG_FILL = -1e30


def rotate(new_keys, lengths):
    positions = (lengths[:, None] + jnp.arange(new_keys.shape[1], dtype=jnp.int32)[None, :]).astype(
        jnp.float32
    )
    half_dim = new_keys.shape[-1] // 2
    inverse = jnp.exp(
        -math.log(ROPE_BASE) * 2.0 * jnp.arange(half_dim, dtype=jnp.float32) / new_keys.shape[-1]
    )
    angles = positions[:, :, None] * inverse[None, None, :]
    cosine_part = jnp.concatenate([jnp.cos(angles), jnp.cos(angles)], -1)[:, :, None, :]
    sine_part = jnp.concatenate([jnp.sin(angles), jnp.sin(angles)], -1)[:, :, None, :]
    rotated = jnp.concatenate([-new_keys[..., half_dim:], new_keys[..., :half_dim]], -1)
    return new_keys * cosine_part + rotated * sine_part


def body(
    grad_parts,
    master,
    moment_one,
    moment_two,
    hidden_in,
    queries,
    cache_keys,
    cache_values,
    cache_lengths,
):
    col_width = master.shape[1]
    grad_sum = lax.psum_scatter(grad_parts[0], "tp", scatter_dimension=1, tiled=True)
    squares = lax.psum(jnp.sum(grad_sum * grad_sum), ("grp", "rep", "tp"))
    norm_limit = math.sqrt(D * 2 * KVH * HD)
    clipped = grad_sum * jnp.minimum(1.0, norm_limit / jnp.sqrt(squares))
    new_moment_one = BETA_ONE * moment_one + (1.0 - BETA_ONE) * clipped
    new_moment_two = BETA_TWO * moment_two + (1.0 - BETA_TWO) * clipped * clipped
    update = new_moment_one / FIRST_CORR / (jnp.sqrt(new_moment_two / SECOND_CORR) + EPSILON)
    weights = (master - LEARN_RATE * update).astype(jnp.bfloat16)
    row_count, step_count, model_width = hidden_in.shape
    token_count = row_count * step_count
    flat_inputs = hidden_in.reshape(token_count, model_width)
    sliced = lax.all_to_all(
        lax.all_to_all(flat_inputs, "grp", split_axis=1, concat_axis=0, tiled=True),
        "rep",
        split_axis=1,
        concat_axis=0,
        tiled=True,
    )
    group_count = lax.axis_size("grp")
    replica_count = lax.axis_size("rep")
    ordered = sliced.reshape(replica_count, group_count, token_count, weights.shape[0])
    ordered = jnp.swapaxes(ordered, 0, 1).reshape(
        group_count * replica_count * token_count, weights.shape[0]
    )
    projected = lax.psum_scatter(
        jnp.dot(ordered, weights, preferred_element_type=jnp.float32),
        ("grp", "rep"),
        scatter_dimension=0,
        tiled=True,
    )
    heads_here = col_width // (2 * HD)
    projected = projected.reshape(row_count, step_count, heads_here, 2, HD)
    new_keys = rotate(projected[:, :, :, 0, :], cache_lengths).astype(jnp.bfloat16)
    new_values = projected[:, :, :, 1, :].astype(jnp.bfloat16)
    new_entries = jnp.stack([new_keys, new_values], 3).reshape(row_count, step_count, col_width)
    groups = QH // KVH
    slots = cache_keys.shape[1]
    query_heads = queries.reshape(row_count, step_count, heads_here, groups, HD)
    old_k = cache_keys.reshape(row_count, slots, heads_here, HD)
    old_v = cache_values.reshape(row_count, slots, heads_here, HD)
    scaling = 1.0 / math.sqrt(HD)
    old_scores = (
        jnp.einsum("rsagd,rjad->rsagj", query_heads, old_k, preferred_element_type=jnp.float32)
        * scaling
    )
    valid_slots = jnp.arange(slots, dtype=jnp.int32)[None, :] < cache_lengths[:, None]
    old_scores = jnp.where(valid_slots[:, None, None, None, :], old_scores, NEG_FILL)
    new_scores = (
        jnp.einsum("rsagd,rtad->rsagt", query_heads, new_keys, preferred_element_type=jnp.float32)
        * scaling
    )
    causal = jnp.arange(step_count)[:, None] >= jnp.arange(step_count)[None, :]
    new_scores = jnp.where(causal[None, :, None, None, :], new_scores, NEG_FILL)
    scores = jnp.concatenate([old_scores, new_scores], -1)
    row_max = jnp.max(scores, -1, keepdims=True)
    exp_scores = jnp.exp(scores - row_max)
    probs = (exp_scores / jnp.sum(exp_scores, -1, keepdims=True)).astype(jnp.bfloat16)
    output = jnp.einsum(
        "rsagj,rjad->rsagd", probs[..., :slots], old_v, preferred_element_type=jnp.float32
    )
    output = output + jnp.einsum(
        "rsagt,rtad->rsagd", probs[..., slots:], new_values, preferred_element_type=jnp.float32
    )
    attended = output.reshape(row_count, step_count, heads_here * groups * HD).astype(jnp.bfloat16)
    return (new_moment_one, new_moment_two, new_entries, attended)


def solution(mesh):
    placed = (
        P("tp", ("grp", "rep"), None),
        P(("grp", "rep"), "tp"),
        P(("grp", "rep"), "tp"),
        P(("grp", "rep"), "tp"),
        P(("grp", "rep"), None, None),
        P(("grp", "rep"), None, "tp"),
        P(("grp", "rep"), None, "tp"),
        P(("grp", "rep"), None, "tp"),
        P(("grp", "rep")),
    )
    return jax.shard_map(
        body,
        mesh=mesh,
        in_specs=placed,
        out_specs=(
            P(("grp", "rep"), "tp"),
            P(("grp", "rep"), "tp"),
            P(("grp", "rep"), None, "tp"),
            P(("grp", "rep"), None, "tp"),
        ),
        check_vma=False,
    )
```

profile of v0, /device:TPU:0, one launch (start us, length us, event | category | flops | bytes accessed | tf_op | source)
XLA Modules:
  0.0 188.0 jit_solution(10694782064445248935)
XLA Ops:
  7.2 0.0 reduce-scatter.5.cloned.1.call-start
  7.2 0.0 copy-start.4
  7.2 0.0 copy-start.6
  7.2 0.0 copy-start.1
  7.2 0.7 reduce-scatter.5.cloned.1.call-update
  7.9 0.2 copy-done.4
  8.1 0.1 all_to_all.24
  8.2 0.7 copy.47
  8.9 4.2 %all-to-all-start = ((bf16[16,2,2560]{2,0,1:T(8,128)(2,1)}), bf16[16,2,2560]{2,0,1:T(8,128)(2,1)S(1)}, u32[]{:S(2)}, u32[]{:S(2)}) async-start(bf16[16,2,2560]{2,0,1:T(8,128)(2,1)} %copy.47), calls=%async_computation.1 | async-start | bytes 327680 | tf_op jit(solution)/shard_map/all_to_all | solution.py:63
  13.1 0.0 copy-done.6
  13.2 0.0 copy-done.1
  13.2 2.1 %reshape.137 = bf16[4,1024,2,128]{3,2,1,0:T(2,128)(2,1)} reshape(bf16[4,1024,256]{2,1,0:T(8,128)(2,1)S(1)} %copy-done.1) | data formatting | bytes 4194304 | tf_op jit(solution)/shard_map/reshape | solution.py:89
  15.2 2.6 %reshape.139 = bf16[4,1024,2,128]{3,2,1,0:T(2,128)(2,1)S(1)} reshape(bf16[4,1024,256]{2,1,0:T(8,128)(2,1)} %param.16) | data formatting | bytes 4194304 | tf_op jit(solution)/shard_map/reshape | solution.py:90
  17.8 0.0 copy-done.7
  17.8 0.1 add_convert_fusion
  17.9 0.1 multiply_cosine_fusion
  18.0 0.1 pad_maximum_fusion.1
  18.1 0.0 all-to-all-done
  18.2 0.7 copy.48
  18.9 5.6 %all-to-all-start.1 = ((bf16[32,4,640]{2,0,1:T(8,128)(2,1)}), bf16[32,4,640]{2,0,1:T(8,128)(2,1)}, u32[]{:S(2)}, u32[]{:S(2)}) async-start(bf16[32,4,640]{2,0,1:T(8,128)(2,1)} %copy.48), calls=%async_computation.2 | async-start | bytes 327680 | tf_op jit(solution)/shard_map/all_to_all | solution.py:62
  24.4 40.0 %reduce-scatter.5.cloned.1.call-done = f32[640,512]{1,0:T(8,128)} async-done(((f32[640,2048]{1,0:T(8,128)}), f32[640,512]{1,0:T(8,128)}) %reduce-scatter.5.cloned.1.call-update) | async-done | bytes 1310736 | tf_op jit(solution)/shard_map/reduce_scatter | solution.py:51
  64.4 2.4 %multiply_reduce_fusion = f32[]{:T(128)} fusion(f32[640,512]{1,0:T(8,128)} %reduce-scatter.5.cloned.1.call-done), kind=kLoop, calls=%fused_computation.11 | loop fusion | flops 655359 | bytes 1310724 | tf_op jit(solution)/shard_map/reduce_sum | solution.py:52
  66.8 0.0 all-to-all-done.1
  66.8 1.6 copy.49
  68.4 39.5 %psum.7 = f32[]{:T(128)} all-reduce(f32[]{:T(128)} %multiply_reduce_fusion), channel_id=1, replica_groups=mesh['grp'=2,'rep'=4,'tp'=4] {'grp','rep','tp'}, use_global_device_ids=true, to_apply=%region_2.0 | all-reduce | flops 1 | bytes 8 | tf_op jit(solution)/shard_map/psum | solution.py:52
  108.6 0.0 copy-start.8
  108.6 2.3 %fusion.13 = (f32[640,512]{1,0:T(8,128)S(1)}, f32[640,512]{1,0:T(8,128)S(1)}) fusion(f32[640,512]{1,0:T(8,128)} %param.12, f32[640,512]{1,0:T(8,128)S(1)} %copy-done, f32[]{:T(128)S(6)} %min_shard_map.3, f32[640,512]{1,0:T(8,128)} %param.11), kind=kLoop, calls=%fused_computation.8 | loop fusion | flops 2621440 | bytes 6553604 | tf_op jit(solution)/shard_map/add | solution.py:56
  110.9 0.0 copy-start.2
  110.9 0.0 copy-start.3
  110.9 1.0 copy-done.2
  112.0 0.4 copy-done.3
  112.4 0.0 copy-done.5
  112.4 0.8 convolution_bitcast_fusion
  113.2 0.8 copy.71
  114.1 0.0 reduce-scatter.7.cloned.1.call-update
  114.1 0.1 iota_compare_fusion
  114.2 2.5 %fusion.45 = (f32[4,4,2,5]{3,1,2,0:T(4,128)S(1)}, f32[4,4,2,5,1024]{4,3,1,2,0:T(8,128)S(1)}) fusion(bf16[4,4,2,5,128]{4,3,2,1,0:T(8,128)(2,1)S(1)} %reshape.138, bf16[4,1024,2,128,1]{3,2,1,0,4:T(2,128)(2,1)} %bitcast.56, pred[4,1024]{1,0:T(4,128)(4,1)S(1)} %iota_compare_fusion), kind=kOutput, calls=%fused_computation.56 | convolution fusion | flops 42434400 | bytes 2798208 | tf_op jit(solution)/shard_map/rsagd,rjad->rsagj/dot_general | solution.py:93
  116.6 60.5 %reduce-scatter.7.cloned.1.call-done = f32[16,512]{1,0:T(8,128)} async-done(((f32[128,512]{1,0:T(8,128)}), f32[16,512]{1,0:T(8,128)}) %reduce-scatter.7.cloned.1.call-update) | async-done | bytes 32784 | tf_op jit(solution)/shard_map/reduce_scatter | solution.py:75
  177.2 0.8 reshape.135
  178.0 0.1 slice_negate_fusion
  178.1 0.1 fusion.32
  178.2 0.6 copy.53
  178.8 0.3 fusion.46
  179.2 0.4 fusion.26
  179.6 0.3 divide_convert_fusion
  179.9 0.1 convolution_bitcast_fusion.1
  180.0 0.5 fusion.23
  180.5 0.7 convert_element_type.40
  (17 shorter events, 0.2 us)
Async XLA Ops:
  7.2 57.3 %reduce-scatter.5.cloned.1.call-start = ((), (), s32[]{:S(2)}) async-start(), calls=%async_computation.4 | async-start | bytes 6553600 | tf_op jit(solution)/shard_map/reduce_scatter | solution.py:51
  7.2 0.9 copy-start.4
  7.2 5.9 %copy-start.6 = (bf16[4,4,1280]{2,1,0:T(4,128)(2,1)S(1)}, bf16[4,4,1280]{2,1,0:T(4,128)(2,1)}, u32[]{:S(2)}) copy-start(bf16[4,4,1280]{2,1,0:T(4,128)(2,1)} %param.14) | copy-start | bytes 122884
  7.2 5.9 %copy-start.1 = (bf16[4,1024,256]{2,1,0:T(8,128)(2,1)S(1)}, bf16[4,1024,256]{2,1,0:T(8,128)(2,1)}, u32[]{:S(2)}) copy-start(bf16[4,1024,256]{2,1,0:T(8,128)(2,1)} %param.15) | copy-start | bytes 6291460
  8.9 9.2 %all-to-all-start = ((bf16[16,2,2560]{2,0,1:T(8,128)(2,1)}), bf16[16,2,2560]{2,0,1:T(8,128)(2,1)S(1)}, u32[]{:S(2)}, u32[]{:S(2)}) async-start(bf16[16,2,2560]{2,0,1:T(8,128)(2,1)} %copy.47), calls=%async_computation.1 | async-start | bytes 327680 | tf_op jit(solution)/shard_map/all_to_all | solution.py:63
  15.2 2.6 %copy-start.7 = (s32[4]{0:T(128)S(1)}, s32[4]{0:T(128)}, u32[]{:S(2)}) copy-start(s32[4]{0:T(128)} %param.17) | copy-start | bytes 52
  18.9 47.9 %all-to-all-start.1 = ((bf16[32,4,640]{2,0,1:T(8,128)(2,1)}), bf16[32,4,640]{2,0,1:T(8,128)(2,1)}, u32[]{:S(2)}, u32[]{:S(2)}) async-start(bf16[32,4,640]{2,0,1:T(8,128)(2,1)} %copy.48), calls=%async_computation.2 | async-start | bytes 327680 | tf_op jit(solution)/shard_map/all_to_all | solution.py:62
  24.4 152.7 %reduce-scatter.7.cloned.1.call-start = ((), (), s32[]{:S(2)}) async-start(), calls=%async_computation.5 | async-start | bytes 294912 | tf_op jit(solution)/shard_map/reduce_scatter | solution.py:75
  64.4 44.1 %copy-start = (f32[640,512]{1,0:T(8,128)S(1)}, f32[640,512]{1,0:T(8,128)}, u32[]{:S(2)}) copy-start(f32[640,512]{1,0:T(8,128)} %reduce-scatter.5.cloned.1.call-done) | copy-start | bytes 3932164
  108.6 3.8 %copy-start.5 = (bf16[2,4,16,640]{3,2,1,0:T(8,128)(2,1)S(1)}, bf16[2,4,16,640]{3,2,1,0:T(8,128)(2,1)}, u32[]{:S(2)}) copy-start(bf16[2,4,16,640]{3,2,1,0:T(8,128)(2,1)} %copy.49) | copy-start | bytes 491524
  108.6 3.8 %copy-start.8 = (f32[640,512]{1,0:T(8,128)S(1)}, f32[640,512]{1,0:T(8,128)}, u32[]{:S(2)}) copy-start(f32[640,512]{1,0:T(8,128)} %param.10) | copy-start | bytes 3932164
  110.9 1.1 copy-start.2
  110.9 1.5 copy-start.3
Sparse Core Ops, SparseCore 0:
  10.5 53.8 reduce-scatter.4
  114.2 62.9 reduce-scatter.6
where the time goes:
time: 189 us; the launch traced here: 188 us
  waiting for transfers between devices  101 us (53%)
  blocking collectives  39.5 us (21%)
  between operations  14.9 us (8%)
  local copies, waits for them, and re-layouts  12.4 us (7%)
  starting transfers between devices  9.83 us (5%)
  other arithmetic  5.93 us (3%)
  matrix products  4.22 us (2%)
    reduce_scatter x1, waiting for transfers between devices, body(): lax.psum_scatter(jnp.dot(ordered, weights, preferred_element_type=jnp.flo...  60.5 us
    reduce_scatter x1, waiting for transfers between devices, body(): lax.psum_scatter(grad_parts[0], 'tp', scatter_dimension=1, tiled=True)  40 us
    psum x1, blocking collectives, body(): squares = lax.psum(jnp.sum(grad_sum * grad_sum), ('grp', 'rep', 'tp'))  39.5 us
    all_to_all x1, starting transfers between devices, body(): lax.all_to_all(lax.all_to_all(flat_inputs, 'grp', split_axis=1, concat_ax...  5.56 us
    all_to_all x1, starting transfers between devices, body(): lax.all_to_all(flat_inputs, 'grp', split_axis=1, concat_axis=0, tiled=True)  4.23 us
  transfers between devices with their start and end apart: 4, of which 2 were waited for; matrix products, arithmetic and copies ran while one was open for 6% of the time, Pallas kernels for 0%

commit v1 on v0

--- a/solution.py
+++ b/solution.py
@@ -1,8 +1,11 @@
+import functools
 import math
 
 import jax
 import jax.numpy as jnp
 from jax import lax
+from jax.experimental import pallas as pl
+from jax.experimental.pallas import tpu as pltpu
 from jax.sharding import PartitionSpec as P
 
 D = 5120
@@ -115,7 +118,429 @@
     return (new_moment_one, new_moment_two, new_entries, attended)
 
 
+MESH = pl.DeviceIdType.MESH
+CHUNK = 64
+PAD = 32
+
+
+def fused_kernel(
+    sizes,
+    lengths_ref,
+    cos_ref,
+    sin_ref,
+    hidden_ref,
+    queries_ref,
+    grad_ref,
+    master_ref,
+    one_ref,
+    two_ref,
+    keys_ref,
+    values_ref,
+    one_out,
+    two_out,
+    entries_out,
+    attended_out,
+    fwd_own,
+    fwd_mate,
+    sum_own,
+    sum_mate,
+    fwd_send,
+    sum_far,
+    grad_total,
+    master_v,
+    one_v,
+    two_v,
+    keys_v,
+    values_v,
+    hidden_in_v,
+    hidden_f,
+    weights_v,
+    squares_send,
+    squares_all,
+    proj_send,
+    proj_recv,
+    query_f,
+    old_max,
+    old_sum,
+    old_out,
+    local_sem,
+    mate_send_sem,
+    mate_recv_sem,
+    far_send_sem,
+    far_recv_sem,
+    hid_send_sem,
+    hid_recv_sem,
+    sq_send_sem,
+    sq_recv_sem,
+    proj_send_sem,
+    proj_recv_sem,
+    load_sem,
+    cache_sem,
+    out_sem,
+):
+    ngrp, nrep, ntp = sizes
+    ngroup = ngrp * nrep
+    ndev = ngroup * ntp
+    rows, cols = master_ref.shape
+    nrow, nstep, width = hidden_ref.shape
+    tokens = nrow * nstep
+    slots = keys_ref.shape[1]
+    heads = cols // (2 * HD)
+    groups = QH // KVH
+    nchunk = rows // CHUNK
+    scaling = 1.0 / math.sqrt(HD)
+
+    g = lax.axis_index("grp")
+    r = lax.axis_index("rep")
+    t = lax.axis_index("tp")
+    p = g * nrep + r
+    flat = p * ntp + t
+    y = t // 2
+    c = t % 2
+    mate = y * 2 + (1 - c)
+    far = (1 - y) * 2 + c
+    far_mate = (1 - y) * 2 + (1 - c)
+
+    def flat_id(k):
+        f = lax.rem(flat + k, ndev)
+        q = f // ntp
+        return {"grp": q // nrep, "rep": lax.rem(q, nrep), "tp": lax.rem(f, ntp)}
+
+    def group_id(k):
+        q = lax.rem(p + k, ngroup)
+        return {"grp": q // nrep, "rep": lax.rem(q, nrep)}
+
+    barrier = pltpu.get_barrier_semaphore()
+
+    def greet(k, carry):
+        pl.semaphore_signal(barrier, inc=1, device_id=flat_id(k), device_id_type=MESH)
+        return carry
+
+    lax.fori_loop(1, ndev, greet, 0)
+
+    def block(i, owner):
+        return grad_ref.at[0, pl.ds(pl.multiple_of(i * CHUNK, CHUNK), CHUNK), pl.ds(pl.multiple_of(owner * cols, cols), cols)]
+
+    def at_rows(ref, i):
+        return ref.at[pl.ds(pl.multiple_of(i * CHUNK, CHUNK), CHUNK)]
+
+    def local_copy(which, i):
+        owner, dst = ((far, fwd_own), (t, sum_own))[which]
+        return pltpu.make_async_copy(block(i, owner), at_rows(dst, i), local_sem.at[which, i])
+
+    def mate_copy(which, i):
+        owner, dst = ((far_mate, fwd_mate), (mate, sum_mate))[which]
+        return pltpu.make_async_remote_copy(
+            src_ref=block(i, owner),
+            dst_ref=at_rows(dst, i),
+            send_sem=mate_send_sem.at[which, i],
+            recv_sem=mate_recv_sem.at[which, i],
+            device_id={"tp": mate},
+            device_id_type=MESH,
+        )
+
+    def far_copy(i):
+        return pltpu.make_async_remote_copy(
+            src_ref=at_rows(fwd_send, i),
+            dst_ref=at_rows(sum_far, i),
+            send_sem=far_send_sem.at[i],
+            recv_sem=far_recv_sem.at[i],
+            device_id={"tp": far},
+            device_id_type=MESH,
+        )
+
+    def hid_copy(k):
+        q = lax.rem(p + k, ngroup)
+        return pltpu.make_async_remote_copy(
+            src_ref=hidden_ref.at[:, :, pl.ds(pl.multiple_of(q * rows, 128), rows)],
+            dst_ref=hidden_in_v.at[k - 1],
+            send_sem=hid_send_sem.at[k - 1],
+            recv_sem=hid_recv_sem.at[k - 1],
+            device_id=group_id(k),
+            device_id_type=MESH,
+        )
+
+    def sq_copy(k):
+        return pltpu.make_async_remote_copy(
+            src_ref=squares_send,
+            dst_ref=squares_all.at[k],
+            send_sem=sq_send_sem.at[k],
+            recv_sem=sq_recv_sem.at[k],
+            device_id=flat_id(k),
+            device_id_type=MESH,
+        )
+
+    def proj_copy(k):
+        return pltpu.make_async_remote_copy(
+            src_ref=proj_send.at[pl.ds(k * tokens, tokens)],
+            dst_ref=proj_recv.at[k - 1],
+            send_sem=proj_send_sem.at[k - 1],
+            recv_sem=proj_recv_sem.at[k - 1],
+            device_id=group_id(ngroup - k),
+            device_id_type=MESH,
+        )
+
+    def each(count, fn, start=0):
+        def step(i, carry):
+            fn(i)
+            return carry
+
+        lax.fori_loop(start, count, step, 0)
+
+    each(nchunk, lambda i: local_copy(0, i).start())
+
+    pl.semaphore_wait(barrier, ndev - 1)
+
+    each(nchunk, lambda i: mate_copy(0, i).start())
+    each(nchunk, lambda i: mate_copy(1, i).start())
+    for k in range(1, ngroup):
+        hid_copy(k).start()
+    keys_copies = [pltpu.make_async_copy(keys_ref.at[i], keys_v.at[i], cache_sem.at[0, i]) for i in range(nrow)]
+    values_copies = [pltpu.make_async_copy(values_ref.at[i], values_v.at[i], cache_sem.at[1, i]) for i in range(nrow)]
+    for i in range(nrow):
+        keys_copies[i].start()
+        values_copies[i].start()
+    each(nchunk, lambda i: local_copy(1, i).start())
+    loads = [
+        pltpu.make_async_copy(src, dst, load_sem.at[i])
+        for i, (src, dst) in enumerate(((master_ref, master_v), (one_ref, one_v), (two_ref, two_v)))
+    ]
+    for copy in loads:
+        copy.start()
+
+    query_f[...] = jnp.zeros_like(query_f)
+    for i in range(nrow):
+        row_q = queries_ref[i].astype(jnp.float32)
+        for a in range(heads):
+            for j in range(groups):
+                n = a * groups + j
+                query_f[a, i * PAD + j * nstep : i * PAD + (j + 1) * nstep, :] = row_q[:, n * HD : (n + 1) * HD]
+
+    def forward(i):
+        local_copy(0, i).wait()
+        mate_copy(0, i).wait_recv()
+        at_rows(fwd_send, i)[...] = (at_rows(fwd_own, i)[...] + at_rows(fwd_mate, i)[...]).astype(jnp.bfloat16)
+        far_copy(i).start()
+
+    each(nchunk, forward)
+
+    slot = lax.broadcasted_iota(jnp.int32, (PAD, slots), 1)
+    for i in range(nrow):
+        keys_copies[i].wait()
+        values_copies[i].wait()
+        valid = slot < lengths_ref[i]
+        for a in range(heads):
+            q = query_f[a, i * PAD : (i + 1) * PAD, :].astype(jnp.bfloat16)
+            scores = lax.dot_general(
+                q,
+                keys_v[i, :, a * HD : (a + 1) * HD],
+                (((1,), (1,)), ((), ())),
+                preferred_element_type=jnp.float32,
+            )
+            scores = jnp.where(valid, scores * scaling, NEG_FILL)
+            top = jnp.max(scores, -1, keepdims=True)
+            e = jnp.exp(scores - top)
+            here = slice(i * PAD, (i + 1) * PAD)
+            old_max[a, here, :] = jnp.broadcast_to(top, (PAD, HD))
+            old_sum[a, here, :] = jnp.broadcast_to(jnp.sum(e, -1, keepdims=True), (PAD, HD))
+            old_out[a, here, :] = jnp.dot(
+                e.astype(jnp.bfloat16), values_v[i, :, a * HD : (a + 1) * HD], preferred_element_type=jnp.float32
+            )
+
+    for k in range(ngroup):
+        if k == 0:
+            own = hidden_ref[:, :, pl.ds(pl.multiple_of(p * rows, 128), rows)]
+        else:
+            hid_copy(k).wait_recv()
+            own = hidden_in_v[k - 1]
+        for i in range(nrow):
+            at = k * tokens + i * nstep
+            hidden_f[at : at + nstep, :] = own[i].astype(jnp.float32)
+
+    def total(i, acc):
+        local_copy(1, i).wait()
+        mate_copy(1, i).wait_recv()
+        far_copy(i).wait_recv()
+        s = at_rows(sum_own, i)[...] + at_rows(sum_mate, i)[...] + at_rows(sum_far, i)[...].astype(jnp.float32)
+        at_rows(grad_total, i)[...] = s
+        return acc + jnp.sum((s * s).reshape(CHUNK // 8, 8, cols), axis=0)
+
+    acc = lax.fori_loop(0, nchunk, total, jnp.zeros((8, cols), jnp.float32))
+    part = jnp.sum(acc, axis=0, keepdims=True)
+    mine = sum(part[:, j * 128 : (j + 1) * 128] for j in range(cols // 128))
+    squares_send[...] = mine
+    each(ndev, lambda k: sq_copy(k).start(), 1)
+    squares_all[0] = mine
+    for copy in loads:
+        copy.wait()
+    each(ndev, lambda k: sq_copy(k).wait_recv(), 1)
+    squares = jnp.sum(jnp.sum(squares_all[...], axis=0), axis=1, keepdims=True)
+    norm_limit = math.sqrt(D * 2 * KVH * HD)
+    factor = jnp.minimum(1.0, norm_limit / jnp.sqrt(jnp.broadcast_to(squares, (1, cols))))
+
+    def adam(i):
+        clipped = at_rows(grad_total, i)[...] * factor
+        one = BETA_ONE * at_rows(one_v, i)[...] + (1.0 - BETA_ONE) * clipped
+        two = BETA_TWO * at_rows(two_v, i)[...] + (1.0 - BETA_TWO) * clipped * clipped
+        at_rows(one_v, i)[...] = one
+        at_rows(two_v, i)[...] = two
+        update = (one * (LEARN_RATE / FIRST_CORR)) / (jnp.sqrt(two * (1.0 / SECOND_CORR)) + EPSILON)
+        at_rows(weights_v, i)[...] = (at_rows(master_v, i)[...] - update).astype(jnp.bfloat16)
+
+    each(nchunk, adam)
+    proj_send[...] = jnp.dot(hidden_f[...].astype(jnp.bfloat16), weights_v[...], preferred_element_type=jnp.float32)
+    for k in range(1, ngroup):
+        proj_copy(k).start()
+    outs = [
+        pltpu.make_async_copy(one_v, one_out, out_sem.at[0]),
+        pltpu.make_async_copy(two_v, two_out, out_sem.at[1]),
+    ]
+    for copy in outs:
+        copy.start()
+
+    each(nchunk, lambda i: mate_copy(0, i).wait_send())
+    each(nchunk, lambda i: mate_copy(1, i).wait_send())
+    each(nchunk, lambda i: far_copy(i).wait_send())
+    each(ndev, lambda k: sq_copy(k).wait_send(), 1)
+    for k in range(1, ngroup):
+        hid_copy(k).wait_send()
+
+    projected = proj_send[0:tokens, :]
+    for k in range(1, ngroup):
+        proj_copy(k).wait_recv()
+        projected = projected + proj_recv[k - 1]
+
+    qi = lax.broadcasted_iota(jnp.int32, (nrow * PAD, tokens), 0)
+    kj = lax.broadcasted_iota(jnp.int32, (nrow * PAD, tokens), 1)
+    seen = (qi // PAD == kj // nstep) & (qi % nstep >= kj % nstep)
+    for a in range(heads):
+        k = projected[:, 2 * a * HD : (2 * a + 1) * HD]
+        new_k = (k * cos_ref[...] + pltpu.roll(k, HD // 2, 1) * sin_ref[...]).astype(jnp.bfloat16)
+        new_v = projected[:, (2 * a + 1) * HD : (2 * a + 2) * HD].astype(jnp.bfloat16)
+        entries_out[:, 2 * a * HD : (2 * a + 1) * HD] = new_k.astype(jnp.float32)
+        entries_out[:, (2 * a + 1) * HD : (2 * a + 2) * HD] = new_v.astype(jnp.float32)
+        scores = lax.dot_general(
+            query_f[a].astype(jnp.bfloat16), new_k, (((1,), (1,)), ((), ())), preferred_element_type=jnp.float32
+        )
+        scores = jnp.where(seen, scores * scaling, NEG_FILL)
+        before = old_max[a][:, 0:1]
+        top = jnp.maximum(before, jnp.max(scores, -1, keepdims=True))
+        alpha = jnp.exp(before - top)
+        e = jnp.exp(scores - top)
+        whole = old_sum[a][:, 0:1] * alpha + jnp.sum(e, -1, keepdims=True)
+        o = old_out[a] * alpha + jnp.dot(e.astype(jnp.bfloat16), new_v, preferred_element_type=jnp.float32)
+        old_out[a] = o / whole
+        for i in range(nrow):
+            for j in range(groups):
+                n = a * groups + j
+                at = i * PAD + j * nstep
+                attended_out[i, :, n * HD : (n + 1) * HD] = old_out[a, at : at + nstep, :]
+
+    for k in range(1, ngroup):
+        proj_copy(k).wait_send()
+    for copy in outs:
+        copy.wait()
+
+
+def fused_body(
+    sizes,
+    grad_parts,
+    master,
+    moment_one,
+    moment_two,
+    hidden_in,
+    queries,
+    cache_keys,
+    cache_values,
+    cache_lengths,
+):
+    ngrp, nrep, ntp = sizes
+    ngroup = ngrp * nrep
+    ndev = ngroup * ntp
+    rows, cols = master.shape
+    nrow, nstep, width = hidden_in.shape
+    tokens = nrow * nstep
+    slots = cache_keys.shape[1]
+    heads = cols // (2 * HD)
+    nchunk = rows // CHUNK
+    half = HD // 2
+    inverse = jnp.exp(-math.log(ROPE_BASE) * 2.0 * jnp.arange(half, dtype=jnp.float32) / HD)
+    positions = (cache_lengths[:, None] + jnp.arange(nstep, dtype=jnp.int32)[None, :]).astype(jnp.float32)
+    angles = positions.reshape(tokens, 1) * inverse[None, :]
+    cos = jnp.concatenate([jnp.cos(angles)] * 2, -1)
+    sin = jnp.concatenate([-jnp.sin(angles), jnp.sin(angles)], -1)
+    f32, bf16 = jnp.float32, jnp.bfloat16
+    vm = pltpu.VMEM
+    dma = pltpu.SemaphoreType.DMA
+    vmem = pl.BlockSpec(memory_space=pltpu.VMEM)
+    hbm = pl.BlockSpec(memory_space=pltpu.HBM)
+    smem = pl.BlockSpec(memory_space=pltpu.SMEM)
+    new_one, new_two, entries, attended = pl.pallas_call(
+        functools.partial(fused_kernel, sizes),
+        out_shape=(
+            jax.ShapeDtypeStruct((rows, cols), f32),
+            jax.ShapeDtypeStruct((rows, cols), f32),
+            jax.ShapeDtypeStruct((tokens, cols), f32),
+            jax.ShapeDtypeStruct(queries.shape, f32),
+        ),
+        in_specs=[smem, vmem, vmem, vmem, vmem] + [hbm] * 6,
+        out_specs=(hbm, hbm, vmem, vmem),
+        scratch_shapes=[
+            vm((rows, cols), f32),
+            vm((rows, cols), f32),
+            vm((rows, cols), f32),
+            vm((rows, cols), f32),
+            vm((rows, cols), bf16),
+            vm((rows, cols), bf16),
+            vm((rows, cols), f32),
+            vm((rows, cols), f32),
+            vm((rows, cols), f32),
+            vm((rows, cols), f32),
+            vm(cache_keys.shape, bf16),
+            vm(cache_values.shape, bf16),
+            vm((ngroup - 1, nrow, nstep, rows), bf16),
+            vm((ngroup * tokens, rows), f32),
+            vm((rows, cols), bf16),
+            vm((1, 128), f32),
+            vm((ndev, 1, 128), f32),
+            vm((ngroup * tokens, cols), f32),
+            vm((ngroup - 1, tokens, cols), f32),
+            vm((heads, nrow * PAD, HD), f32),
+            vm((heads, nrow * PAD, HD), f32),
+            vm((heads, nrow * PAD, HD), f32),
+            vm((heads, nrow * PAD, HD), f32),
+            dma((2, nchunk)),
+            dma((2, nchunk)),
+            dma((2, nchunk)),
+            dma((nchunk,)),
+            dma((nchunk,)),
+            dma((ngroup - 1,)),
+            dma((ngroup - 1,)),
+            dma((ndev,)),
+            dma((ndev,)),
+            dma((ngroup - 1,)),
+            dma((ngroup - 1,)),
+            dma((3,)),
+            dma((2, nrow)),
+            dma((2,)),
+        ],
+        compiler_params=pltpu.CompilerParams(
+            collective_id=0, has_side_effects=True, vmem_limit_bytes=48 * 1024 * 1024
+        ),
+    )(
+        cache_lengths, cos, sin, hidden_in, queries, grad_parts, master, moment_one, moment_two, cache_keys, cache_values
+    )
+    return (
+        new_one,
+        new_two,
+        entries.astype(bf16).reshape(nrow, nstep, cols),
+        attended.astype(bf16),
+    )
+
+
 def solution(mesh):
+    sizes = (mesh.shape["grp"], mesh.shape["rep"], mesh.shape["tp"])
+    fits = sizes[2] == 4 and D % (sizes[0] * sizes[1] * 128) == 0 and (KVH % sizes[2]) == 0
     placed = (
         P("tp", ("grp", "rep"), None),
         P(("grp", "rep"), "tp"),
@@ -128,7 +553,7 @@
         P(("grp", "rep")),
     )
     return jax.shard_map(
-        body,
+        functools.partial(fused_body, sizes) if fits else body,
         mesh=mesh,
         in_specs=placed,
         out_specs=(

time: 189 us -> 52.1 us (0.28)
  waiting for transfers between devices: 101 us -> 0 us
  Pallas kernels: 0 us -> 41.8 us
  blocking collectives: 39.5 us -> 0 us
  between operations: 14.9 us -> 0.66 us
  starting transfers between devices: 9.83 us -> 0 us
  local copies, waits for them, and re-layouts: 12.4 us -> 7.79 us
  other arithmetic: 5.93 us -> 1.57 us
  matrix products: 4.22 us -> 0 us
    reduce_scatter x2 -> x0, waiting for transfers between devices: 101 us -> none  [the longest x1 60.5 us: body(): lax.psum_scatter(jnp.dot(ordered, weights, preferred_element_type=jnp.flo...]
    pallas_call x0 -> x1, Pallas kernels: none -> 41.8 us  [fused_body(): pl.pallas_call(functools.partial(fused_kernel, sizes), out_shape=(jax.Sha...]
    psum x1 -> x0, blocking collectives: 39.5 us -> none  [body(): squares = lax.psum(jnp.sum(grad_sum * grad_sum), ('grp', 'rep', 'tp'))]
    all_to_all x2 -> x0, starting transfers between devices: 9.79 us -> none  [the longest x1 5.56 us: body(): lax.all_to_all(lax.all_to_all(flat_inputs, 'grp', split_axis=1, concat_ax...]
    reshape x4 -> x1, local copies, waits for them, and re-layouts: 5.44 us -> 0.62 us  [fused_body(): entries.astype(bf16).reshape(nrow, nstep, cols)]
    unnamed x21 -> x12, local copies, waits for them, and re-layouts: 2.58 us -> 7.09 us
    dot_general x5 -> x0, matrix products: 4.22 us -> none  [the longest x1 2.47 us: body(): jnp.einsum('rsagd,rjad->rsagj', query_heads, old_k, preferred_element_typ...]
    reduce_sum x2 -> x0, other arithmetic: 2.74 us -> none  [the longest x1 2.36 us: body(): squares = lax.psum(jnp.sum(grad_sum * grad_sum), ('grp', 'rep', 'tp'))]
  transfers between devices with their start and end apart: 4 -> 0, of which waited for: 2 -> 0; matrix products, arithmetic and copies ran while one was open for 6% -> 0% of each run, Pallas kernels for 0% -> 0%
where the time goes in v1:
time: 52.1 us; the launch traced here: 51.8 us
  Pallas kernels  41.8 us (80%)
  local copies, waits for them, and re-layouts  7.79 us (15%)
  other arithmetic  1.57 us (3%)
  between operations  0.66 us (1%)
    pallas_call x1, Pallas kernels, fused_body(): pl.pallas_call(functools.partial(fused_kernel, sizes), out_shape=(jax.Sha...  41.8 us
    unnamed x12, local copies, waits for them, and re-layouts  7.09 us

profile of v1, /device:TPU:0, one launch (start us, length us, event | category | flops | bytes accessed | tf_op | source)
XLA Modules:
  0.0 51.8 jit_solution(4571884754278066283)
XLA Ops:
  0.6 0.7 %add_convert_fusion = f32[4,4]{1,0:T(4,128)S(1)} fusion(s32[4]{0:T(128)} %lengths_ref.1), kind=kLoop, calls=%fused_computation.5 | loop fusion | flops 32 | bytes 80 | tf_op jit(solution)/shard_map/convert_element_type | solution.py:468
  1.4 0.1 convert_element_type.17
  1.5 0.1 fusion
  1.6 0.1 pad_maximum_fusion
  1.7 0.0 copy-start
  1.7 1.3 %copy-done = f32[640,512]{1,0:T(8,128)S(1)} copy-done((f32[640,512]{1,0:T(8,128)S(1)}, f32[640,512]{1,0:T(8,128)}, u32[]{:S(2)}) %copy-start) | copy-done | bytes 1310744
  3.0 0.0 copy-start.1
  3.0 1.3 %copy-done.1 = f32[640,512]{1,0:T(8,128)S(1)} copy-done((f32[640,512]{1,0:T(8,128)S(1)}, f32[640,512]{1,0:T(8,128)}, u32[]{:S(2)}) %copy-start.1) | copy-done | bytes 1310744
  4.3 0.0 copy-start.2
  4.3 0.9 %copy-done.2 = bf16[4,4,5120]{2,1,0:T(4,128)(2,1)S(1)} copy-done((bf16[4,4,5120]{2,1,0:T(4,128)(2,1)S(1)}, bf16[4,4,5120]{2,1,0:T(4,128)(2,1)}, u32[]{:S(2)}) %copy-start.2) | copy-done | bytes 163864
  5.2 0.0 copy-start.3
  5.2 0.8 %copy-done.3 = bf16[4,4,1280]{2,1,0:T(4,128)(2,1)S(1)} copy-done((bf16[4,4,1280]{2,1,0:T(4,128)(2,1)S(1)}, bf16[4,4,1280]{2,1,0:T(4,128)(2,1)}, u32[]{:S(2)}) %copy-start.3) | copy-done | bytes 40984
  6.0 0.0 copy-start.4
  6.0 0.7 %copy-done.4 = s32[4]{0:T(128)S(1)} copy-done((s32[4]{0:T(128)S(1)}, s32[4]{0:T(128)}, u32[]{:S(2)}) %copy-start.4) | copy-done | bytes 40
  6.6 41.8 %shard_map.120 = (f32[640,512]{1,0:T(8,128)S(1)}, f32[640,512]{1,0:T(8,128)S(1)}, f32[16,512]{1,0:T(8,128)S(1)}, f32[4,4,1280]{2,1,0:T(4,128)S(1)}) custom-call(s32[4]{0:T(128)S(1)} %copy-done.4, f32[16,128]{1,0:T(8,128)S(1)} %get-tuple-element.15.cos_ref, f32[16,128]{1,0:T(8,128)S(1)} %get-tuple-element.16.sin_ref, bf16[4,4,5120]{2,1,0:T(4,128)(2,1)S(1)} %copy-done.2, ...), custom_call_target="tpu_custom_call" | custom-call | tf_op jit(solution)/shard_map/pallas_call | solution.py:478
  48.5 0.6 %reshape.34 = bf16[4,4,512]{2,1,0:T(4,128)(2,1)} reshape(bf16[16,512]{1,0:T(8,128)(2,1)S(1)} %convert_element_type.18) | data formatting | bytes 32768 | tf_op jit(solution)/shard_map/reshape | solution.py:536
  49.1 0.6 %convert_element_type.19 = bf16[4,4,1280]{2,1,0:T(4,128)(2,1)} convert(f32[4,4,1280]{2,1,0:T(4,128)S(1)} %get-tuple-element.11) | non-fusion elementwise | flops 20480 | bytes 122880 | tf_op jit(solution)/shard_map/convert_element_type | solution.py:537
  49.7 1.1 %copy.15 = f32[640,512]{1,0:T(8,128)} copy(f32[640,512]{1,0:T(8,128)S(1)} %get-tuple-element.21) | data formatting | bytes 2621440
  50.8 1.1 %copy.16 = f32[640,512]{1,0:T(8,128)} copy(f32[640,512]{1,0:T(8,128)S(1)} %get-tuple-element.22) | data formatting | bytes 2621440
  (2 shorter events, 0.0 us)
Async XLA Ops:
  1.7 1.3 %copy-start = (f32[640,512]{1,0:T(8,128)S(1)}, f32[640,512]{1,0:T(8,128)}, u32[]{:S(2)}) copy-start(f32[640,512]{1,0:T(8,128)} %master_ref.1) | copy-start | bytes 3932164
  3.0 1.3 %copy-start.1 = (f32[640,512]{1,0:T(8,128)S(1)}, f32[640,512]{1,0:T(8,128)}, u32[]{:S(2)}) copy-start(f32[640,512]{1,0:T(8,128)} %one_ref.1) | copy-start | bytes 3932164
  4.3 0.9 %copy-start.2 = (bf16[4,4,5120]{2,1,0:T(4,128)(2,1)S(1)}, bf16[4,4,5120]{2,1,0:T(4,128)(2,1)}, u32[]{:S(2)}) copy-start(bf16[4,4,5120]{2,1,0:T(4,128)(2,1)} %hidden_ref.1) | copy-start | bytes 491524
  5.2 0.8 %copy-start.3 = (bf16[4,4,1280]{2,1,0:T(4,128)(2,1)S(1)}, bf16[4,4,1280]{2,1,0:T(4,128)(2,1)}, u32[]{:S(2)}) copy-start(bf16[4,4,1280]{2,1,0:T(4,128)(2,1)} %queries_ref.1) | copy-start | bytes 122884
  6.0 0.7 %copy-start.4 = (s32[4]{0:T(128)S(1)}, s32[4]{0:T(128)}, u32[]{:S(2)}) copy-start(s32[4]{0:T(128)} %lengths_ref.1) | copy-start | bytes 52

commit v2 on v1

--- a/solution.py
+++ b/solution.py
@@ -126,8 +126,6 @@
 def fused_kernel(
     sizes,
     lengths_ref,
-    cos_ref,
-    sin_ref,
     hidden_ref,
     queries_ref,
     grad_ref,
@@ -138,8 +136,15 @@
     values_ref,
     one_out,
     two_out,
-    entries_out,
-    attended_out,
+    proj_out,
+    cos_out,
+    sin_out,
+    query_f,
+    old_max,
+    old_sum,
+    old_out,
+    lengths_s,
+    queries_v,
     fwd_own,
     fwd_mate,
     sum_own,
@@ -157,12 +162,9 @@
     weights_v,
     squares_send,
     squares_all,
+    proj_own,
     proj_send,
     proj_recv,
-    query_f,
-    old_max,
-    old_sum,
-    old_out,
     local_sem,
     mate_send_sem,
     mate_recv_sem,
@@ -176,7 +178,7 @@
     proj_recv_sem,
     load_sem,
     cache_sem,
-    out_sem,
+    small_sem,
 ):
     ngrp, nrep, ntp = sizes
     ngroup = ngrp * nrep
@@ -253,7 +255,7 @@
         q = lax.rem(p + k, ngroup)
         return pltpu.make_async_remote_copy(
             src_ref=hidden_ref.at[:, :, pl.ds(pl.multiple_of(q * rows, 128), rows)],
-            dst_ref=hidden_in_v.at[k - 1],
+            dst_ref=hidden_in_v.at[k],
             send_sem=hid_send_sem.at[k - 1],
             recv_sem=hid_recv_sem.at[k - 1],
             device_id=group_id(k),
@@ -272,7 +274,7 @@
 
     def proj_copy(k):
         return pltpu.make_async_remote_copy(
-            src_ref=proj_send.at[pl.ds(k * tokens, tokens)],
+            src_ref=proj_send.at[k - 1],
             dst_ref=proj_recv.at[k - 1],
             send_sem=proj_send_sem.at[k - 1],
             recv_sem=proj_recv_sem.at[k - 1],
@@ -288,6 +290,18 @@
         lax.fori_loop(start, count, step, 0)
 
     each(nchunk, lambda i: local_copy(0, i).start())
+    small = [
+        pltpu.make_async_copy(src, dst, small_sem.at[i])
+        for i, (src, dst) in enumerate(
+            (
+                (lengths_ref, lengths_s),
+                (queries_ref, queries_v),
+                (hidden_ref.at[:, :, pl.ds(pl.multiple_of(p * rows, 128), rows)], hidden_in_v.at[0]),
+            )
+        )
+    ]
+    for copy in small:
+        copy.start()
 
     pl.semaphore_wait(barrier, ndev - 1)
 
@@ -308,9 +322,11 @@
     for copy in loads:
         copy.start()
 
+    for copy in small:
+        copy.wait()
     query_f[...] = jnp.zeros_like(query_f)
     for i in range(nrow):
-        row_q = queries_ref[i].astype(jnp.float32)
+        row_q = queries_v[i].astype(jnp.float32)
         for a in range(heads):
             for j in range(groups):
                 n = a * groups + j
@@ -328,7 +344,7 @@
     for i in range(nrow):
         keys_copies[i].wait()
         values_copies[i].wait()
-        valid = slot < lengths_ref[i]
+        valid = slot < lengths_s[i]
         for a in range(heads):
             q = query_f[a, i * PAD : (i + 1) * PAD, :].astype(jnp.bfloat16)
             scores = lax.dot_general(
@@ -348,14 +364,22 @@
             )
 
     for k in range(ngroup):
-        if k == 0:
-            own = hidden_ref[:, :, pl.ds(pl.multiple_of(p * rows, 128), rows)]
-        else:
+        if k > 0:
             hid_copy(k).wait_recv()
-            own = hidden_in_v[k - 1]
+        own = hidden_in_v[k]
         for i in range(nrow):
             at = k * tokens + i * nstep
             hidden_f[at : at + nstep, :] = own[i].astype(jnp.float32)
+
+    token = lax.broadcasted_iota(jnp.int32, (tokens, HD), 0)
+    lane = lax.broadcasted_iota(jnp.int32, (tokens, HD), 1)
+    position = lax.rem(token, nstep)
+    for i in range(nrow):
+        position = position + jnp.where(token // nstep == i, lengths_s[i], 0)
+    pair = lax.rem(lane, HD // 2).astype(jnp.float32)
+    angle = position.astype(jnp.float32) * jnp.exp(-math.log(ROPE_BASE) * 2.0 * pair / HD)
+    cos_out[...] = jnp.cos(angle)
+    sin_out[...] = jnp.where(lane < HD // 2, -jnp.sin(angle), jnp.sin(angle))
 
     def total(i, acc):
         local_copy(1, i).wait()
@@ -382,21 +406,17 @@
         clipped = at_rows(grad_total, i)[...] * factor
         one = BETA_ONE * at_rows(one_v, i)[...] + (1.0 - BETA_ONE) * clipped
         two = BETA_TWO * at_rows(two_v, i)[...] + (1.0 - BETA_TWO) * clipped * clipped
-        at_rows(one_v, i)[...] = one
-        at_rows(two_v, i)[...] = two
+        at_rows(one_out, i)[...] = one
+        at_rows(two_out, i)[...] = two
         update = (one * (LEARN_RATE / FIRST_CORR)) / (jnp.sqrt(two * (1.0 / SECOND_CORR)) + EPSILON)
         at_rows(weights_v, i)[...] = (at_rows(master_v, i)[...] - update).astype(jnp.bfloat16)
 
     each(nchunk, adam)
-    proj_send[...] = jnp.dot(hidden_f[...].astype(jnp.bfloat16), weights_v[...], preferred_element_type=jnp.float32)
+    partial = jnp.dot(hidden_f[...].astype(jnp.bfloat16), weights_v[...], preferred_element_type=jnp.float32)
     for k in range(1, ngroup):
+        proj_send[k - 1] = partial[k * tokens : (k + 1) * tokens].astype(jnp.bfloat16)
         proj_copy(k).start()
-    outs = [
-        pltpu.make_async_copy(one_v, one_out, out_sem.at[0]),
-        pltpu.make_async_copy(two_v, two_out, out_sem.at[1]),
-    ]
-    for copy in outs:
-        copy.start()
+    proj_own[...] = partial[0:tokens]
 
     each(nchunk, lambda i: mate_copy(0, i).wait_send())
     each(nchunk, lambda i: mate_copy(1, i).wait_send())
@@ -405,39 +425,72 @@
     for k in range(1, ngroup):
         hid_copy(k).wait_send()
 
-    projected = proj_send[0:tokens, :]
+    projected = proj_own[...]
     for k in range(1, ngroup):
         proj_copy(k).wait_recv()
-        projected = projected + proj_recv[k - 1]
-
+        projected = projected + proj_recv[k - 1].astype(jnp.float32)
+    proj_out[...] = projected
+    for k in range(1, ngroup):
+        proj_copy(k).wait_send()
+
+
+def finish_kernel(
+    one_ref,
+    two_ref,
+    proj_ref,
+    cos_ref,
+    sin_ref,
+    query_ref,
+    max_ref,
+    sum_ref,
+    old_ref,
+    one_out,
+    two_out,
+    entries_out,
+    attended_out,
+    heads_v,
+    out_sem,
+):
+    outs = [
+        pltpu.make_async_copy(one_ref, one_out, out_sem.at[0]),
+        pltpu.make_async_copy(two_ref, two_out, out_sem.at[1]),
+    ]
+    for copy in outs:
+        copy.start()
+    nrow, nstep, cols = entries_out.shape
+    tokens = nrow * nstep
+    heads = cols // (2 * HD)
+    groups = QH // KVH
+    scaling = 1.0 / math.sqrt(HD)
     qi = lax.broadcasted_iota(jnp.int32, (nrow * PAD, tokens), 0)
     kj = lax.broadcasted_iota(jnp.int32, (nrow * PAD, tokens), 1)
     seen = (qi // PAD == kj // nstep) & (qi % nstep >= kj % nstep)
     for a in range(heads):
-        k = projected[:, 2 * a * HD : (2 * a + 1) * HD]
-        new_k = (k * cos_ref[...] + pltpu.roll(k, HD // 2, 1) * sin_ref[...]).astype(jnp.bfloat16)
-        new_v = projected[:, (2 * a + 1) * HD : (2 * a + 2) * HD].astype(jnp.bfloat16)
-        entries_out[:, 2 * a * HD : (2 * a + 1) * HD] = new_k.astype(jnp.float32)
-        entries_out[:, (2 * a + 1) * HD : (2 * a + 2) * HD] = new_v.astype(jnp.float32)
+        k = proj_ref[:, 2 * a * HD : (2 * a + 1) * HD]
+        k = k * cos_ref[...] + pltpu.roll(k, HD // 2, 1) * sin_ref[...]
+        v = proj_ref[:, (2 * a + 1) * HD : (2 * a + 2) * HD]
+        new_k = k.astype(jnp.bfloat16)
+        new_v = v.astype(jnp.bfloat16)
+        for i in range(nrow):
+            rows_i = slice(i * nstep, (i + 1) * nstep)
+            entries_out[i, :, 2 * a * HD : (2 * a + 1) * HD] = k[rows_i].astype(jnp.bfloat16)
+            entries_out[i, :, (2 * a + 1) * HD : (2 * a + 2) * HD] = v[rows_i].astype(jnp.bfloat16)
         scores = lax.dot_general(
-            query_f[a].astype(jnp.bfloat16), new_k, (((1,), (1,)), ((), ())), preferred_element_type=jnp.float32
+            query_ref[a].astype(jnp.bfloat16), new_k, (((1,), (1,)), ((), ())), preferred_element_type=jnp.float32
         )
         scores = jnp.where(seen, scores * scaling, NEG_FILL)
-        before = old_max[a][:, 0:1]
+        before = max_ref[a][:, 0:1]
         top = jnp.maximum(before, jnp.max(scores, -1, keepdims=True))
         alpha = jnp.exp(before - top)
         e = jnp.exp(scores - top)
-        whole = old_sum[a][:, 0:1] * alpha + jnp.sum(e, -1, keepdims=True)
-        o = old_out[a] * alpha + jnp.dot(e.astype(jnp.bfloat16), new_v, preferred_element_type=jnp.float32)
-        old_out[a] = o / whole
+        whole = sum_ref[a][:, 0:1] * alpha + jnp.sum(e, -1, keepdims=True)
+        o = old_ref[a] * alpha + jnp.dot(e.astype(jnp.bfloat16), new_v, preferred_element_type=jnp.float32)
+        heads_v[a] = o / whole
         for i in range(nrow):
             for j in range(groups):
                 n = a * groups + j
                 at = i * PAD + j * nstep
-                attended_out[i, :, n * HD : (n + 1) * HD] = old_out[a, at : at + nstep, :]
-
-    for k in range(1, ngroup):
-        proj_copy(k).wait_send()
+                attended_out[i, :, n * HD : (n + 1) * HD] = heads_v[a, at : at + nstep, :].astype(jnp.bfloat16)
     for copy in outs:
         copy.wait()
 
@@ -460,32 +513,24 @@
     rows, cols = master.shape
     nrow, nstep, width = hidden_in.shape
     tokens = nrow * nstep
-    slots = cache_keys.shape[1]
     heads = cols // (2 * HD)
     nchunk = rows // CHUNK
-    half = HD // 2
-    inverse = jnp.exp(-math.log(ROPE_BASE) * 2.0 * jnp.arange(half, dtype=jnp.float32) / HD)
-    positions = (cache_lengths[:, None] + jnp.arange(nstep, dtype=jnp.int32)[None, :]).astype(jnp.float32)
-    angles = positions.reshape(tokens, 1) * inverse[None, :]
-    cos = jnp.concatenate([jnp.cos(angles)] * 2, -1)
-    sin = jnp.concatenate([-jnp.sin(angles), jnp.sin(angles)], -1)
     f32, bf16 = jnp.float32, jnp.bfloat16
     vm = pltpu.VMEM
     dma = pltpu.SemaphoreType.DMA
     vmem = pl.BlockSpec(memory_space=pltpu.VMEM)
     hbm = pl.BlockSpec(memory_space=pltpu.HBM)
-    smem = pl.BlockSpec(memory_space=pltpu.SMEM)
-    new_one, new_two, entries, attended = pl.pallas_call(
+    per_head = vm((heads, nrow * PAD, HD), f32)
+    moment = vm((rows, cols), f32)
+    table = vm((tokens, HD), f32)
+    middle = pl.pallas_call(
         functools.partial(fused_kernel, sizes),
-        out_shape=(
-            jax.ShapeDtypeStruct((rows, cols), f32),
-            jax.ShapeDtypeStruct((rows, cols), f32),
-            jax.ShapeDtypeStruct((tokens, cols), f32),
-            jax.ShapeDtypeStruct(queries.shape, f32),
-        ),
-        in_specs=[smem, vmem, vmem, vmem, vmem] + [hbm] * 6,
-        out_specs=(hbm, hbm, vmem, vmem),
+        out_shape=(moment, moment, vm((tokens, cols), f32), table, table) + (per_head,) * 4,
+        in_specs=[hbm] * 9,
+        out_specs=(vmem,) * 9,
         scratch_shapes=[
+            pltpu.SMEM((nrow,), jnp.int32),
+            vm(queries.shape, bf16),
             vm((rows, cols), f32),
             vm((rows, cols), f32),
             vm((rows, cols), f32),
@@ -498,17 +543,14 @@
             vm((rows, cols), f32),
             vm(cache_keys.shape, bf16),
             vm(cache_values.shape, bf16),
-            vm((ngroup - 1, nrow, nstep, rows), bf16),
+            vm((ngroup, nrow, nstep, rows), bf16),
             vm((ngroup * tokens, rows), f32),
             vm((rows, cols), bf16),
             vm((1, 128), f32),
             vm((ndev, 1, 128), f32),
-            vm((ngroup * tokens, cols), f32),
-            vm((ngroup - 1, tokens, cols), f32),
-            vm((heads, nrow * PAD, HD), f32),
-            vm((heads, nrow * PAD, HD), f32),
-            vm((heads, nrow * PAD, HD), f32),
-            vm((heads, nrow * PAD, HD), f32),
+            vm((tokens, cols), f32),
+            vm((ngroup - 1, tokens, cols), bf16),
+            vm((ngroup - 1, tokens, cols), bf16),
             dma((2, nchunk)),
             dma((2, nchunk)),
             dma((2, nchunk)),
@@ -522,20 +564,25 @@
             dma((ngroup - 1,)),
             dma((3,)),
             dma((2, nrow)),
-            dma((2,)),
+            dma((3,)),
         ],
         compiler_params=pltpu.CompilerParams(
-            collective_id=0, has_side_effects=True, vmem_limit_bytes=48 * 1024 * 1024
+            collective_id=0, has_side_effects=True, vmem_limit_bytes=60 * 1024 * 1024 + 320 * 1024
         ),
-    )(
-        cache_lengths, cos, sin, hidden_in, queries, grad_parts, master, moment_one, moment_two, cache_keys, cache_values
-    )
-    return (
-        new_one,
-        new_two,
-        entries.astype(bf16).reshape(nrow, nstep, cols),
-        attended.astype(bf16),
-    )
+    )(cache_lengths, hidden_in, queries, grad_parts, master, moment_one, moment_two, cache_keys, cache_values)
+    return pl.pallas_call(
+        finish_kernel,
+        out_shape=(
+            jax.ShapeDtypeStruct((rows, cols), f32),
+            jax.ShapeDtypeStruct((rows, cols), f32),
+            jax.ShapeDtypeStruct((nrow, nstep, cols), bf16),
+            jax.ShapeDtypeStruct(queries.shape, bf16),
+        ),
+        in_specs=[vmem] * 9,
+        out_specs=(hbm, hbm, vmem, vmem),
+        scratch_shapes=[vm((heads, nrow * PAD, HD), f32), dma((2,))],
+        compiler_params=pltpu.CompilerParams(vmem_limit_bytes=8 * 1024 * 1024),
+    )(*middle)
 
 
 def solution(mesh):

time: 52.1 us -> 41.2 us (0.79)
  local copies, waits for them, and re-layouts: 7.79 us -> 0 us
  other arithmetic: 1.57 us -> 0 us
  Pallas kernels: 41.8 us -> 40.4 us
    unnamed x12 -> x0, local copies, waits for them, and re-layouts: 7.09 us -> none
    pallas_call x1 -> x2, Pallas kernels: 41.8 us -> 40.4 us  [the longest x1 38.3 us: fused_body(): pl.pallas_call(functools.partial(fused_kernel, sizes), out_shape=(moment,...]
    convert_element_type x3 -> x0, other arithmetic: 1.37 us -> none  [the longest x1 0.73 us: fused_body(): (cache_lengths[:, None] + jnp.arange(nstep, dtype=jnp.int32)[None, :]).as...]
    reshape x1 -> x0, local copies, waits for them, and re-layouts: 0.62 us -> none  [fused_body(): entries.astype(bf16).reshape(nrow, nstep, cols)]
where the time goes in v2:
time: 41.2 us; the launch traced here: 41 us
  Pallas kernels  40.4 us (98%)
  between operations  0.64 us (2%)
    pallas_call x1, Pallas kernels, fused_body(): pl.pallas_call(functools.partial(fused_kernel, sizes), out_shape=(moment,...  38.3 us
    pallas_call x1, Pallas kernels, fused_body(): pl.pallas_call(finish_kernel, out_shape=(jax.ShapeDtypeStruct((rows, cols...  2.13 us

profile of v2, /device:TPU:0, one launch (start us, length us, event | category | flops | bytes accessed | tf_op | source)
XLA Modules:
  0.0 41.0 jit_solution(1151380119795944512)
XLA Ops:
  0.6 38.3 %shard_map.120 = (f32[640,512]{1,0:T(8,128)S(1)}, f32[640,512]{1,0:T(8,128)S(1)}, f32[16,512]{1,0:T(8,128)S(1)}, f32[16,128]{1,0:T(8,128)S(1)}, f32[16,128]{1,0:...) custom-call(s32[4]{0:T(128)} %lengths_ref.1, ...), custom_call_target="tpu_custom_call" | custom-call | tf_op jit(solution)/shard_map/pallas_call | solution.py:526
  38.9 2.1 %shard_map.121 = (f32[640,512]{1,0:T(8,128)}, f32[640,512]{1,0:T(8,128)}, bf16[4,4,512]{2,1,0:T(4,128)(2,1)}, bf16[4,4,1280]{2,1,0:T(4,128)(2,1)}) custom-call(f32[640,512]{1,0:T(8,128)S(1)} %get-tuple-element.13.one_ref, f32[640,512]{1,0:T(8,128)S(1)} %get-tuple-element.14.two_ref, f32[16,512]{1,0:T(8,128)S(1)} %get-tuple-element.15.proj_ref, ...), custom_call_target="tpu_custom_call" | custom-call | tf_op jit(solution)/shard_map/pallas_call | solution.py:573

commit v3 on v2

--- a/solution.py
+++ b/solution.py
@@ -179,6 +179,7 @@
     load_sem,
     cache_sem,
     small_sem,
+    round_sem,
 ):
     ngrp, nrep, ntp = sizes
     ngroup = ngrp * nrep
@@ -214,11 +215,14 @@
 
     barrier = pltpu.get_barrier_semaphore()
 
-    def greet(k, carry):
-        pl.semaphore_signal(barrier, inc=1, device_id=flat_id(k), device_id_type=MESH)
-        return carry
-
-    lax.fori_loop(1, ndev, greet, 0)
+    bits = ndev.bit_length() - 1
+
+    def across(b):
+        stride = 1 << b
+        return flat_id(ndev + stride * (1 - 2 * lax.rem(flat // stride, 2)))
+
+    for b in range(bits):
+        pl.semaphore_signal(barrier, inc=1, device_id=across(b), device_id_type=MESH)
 
     def block(i, owner):
         return grad_ref.at[0, pl.ds(pl.multiple_of(i * CHUNK, CHUNK), CHUNK), pl.ds(pl.multiple_of(owner * cols, cols), cols)]
@@ -303,12 +307,10 @@
     for copy in small:
         copy.start()
 
-    pl.semaphore_wait(barrier, ndev - 1)
+    pl.semaphore_wait(barrier, bits)
 
     each(nchunk, lambda i: mate_copy(0, i).start())
     each(nchunk, lambda i: mate_copy(1, i).start())
-    for k in range(1, ngroup):
-        hid_copy(k).start()
     keys_copies = [pltpu.make_async_copy(keys_ref.at[i], keys_v.at[i], cache_sem.at[0, i]) for i in range(nrow)]
     values_copies = [pltpu.make_async_copy(values_ref.at[i], values_v.at[i], cache_sem.at[1, i]) for i in range(nrow)]
     for i in range(nrow):
@@ -338,7 +340,12 @@
         at_rows(fwd_send, i)[...] = (at_rows(fwd_own, i)[...] + at_rows(fwd_mate, i)[...]).astype(jnp.bfloat16)
         far_copy(i).start()
 
-    each(nchunk, forward)
+    for b in range(bits):
+        pl.semaphore_signal(round_sem.at[b], inc=1, device_id=across(b), device_id_type=MESH)
+        each((b + 1) * nchunk // bits, forward, b * nchunk // bits)
+        pl.semaphore_wait(round_sem.at[b], 1)
+    for k in range(1, ngroup):
+        hid_copy(k).start()
 
     slot = lax.broadcasted_iota(jnp.int32, (PAD, slots), 1)
     for i in range(nrow):
@@ -565,6 +572,7 @@
             dma((3,)),
             dma((2, nrow)),
             dma((3,)),
+            pltpu.SemaphoreType.REGULAR((ndev.bit_length() - 1,)),
         ],
         compiler_params=pltpu.CompilerParams(
             collective_id=0, has_side_effects=True, vmem_limit_bytes=60 * 1024 * 1024 + 320 * 1024
@@ -587,7 +595,8 @@
 
 def solution(mesh):
     sizes = (mesh.shape["grp"], mesh.shape["rep"], mesh.shape["tp"])
-    fits = sizes[2] == 4 and D % (sizes[0] * sizes[1] * 128) == 0 and (KVH % sizes[2]) == 0
+    fits = sizes[2] == 4 and D % (sizes[0] * sizes[1] * 128) == 0 and KVH % sizes[2] == 0
+    fits = fits and (sizes[0] * sizes[1]) & (sizes[0] * sizes[1] - 1) == 0
     placed = (
         P("tp", ("grp", "rep"), None),
         P(("grp", "rep"), "tp"),

time: 41.2 us -> 37.9 us (0.920)
  Pallas kernels: 40.4 us -> 37.1 us
    pallas_call x1, Pallas kernels: 38.3 us -> 35 us  [fused_body(): pl.pallas_call(functools.partial(fused_kernel, sizes), out_shape=(moment,...]
where the time goes in v3:
time: 37.9 us; the launch traced here: 37.7 us
  Pallas kernels  37.1 us (98%)
  between operations  0.64 us (2%)
    pallas_call x1, Pallas kernels, fused_body(): pl.pallas_call(functools.partial(fused_kernel, sizes), out_shape=(moment,...  35 us
    pallas_call x1, Pallas kernels, fused_body(): pl.pallas_call(finish_kernel, out_shape=(jax.ShapeDtypeStruct((rows, cols...  2.13 us

profile of v3, /device:TPU:0, one launch (start us, length us, event | category | flops | bytes accessed | tf_op | source)
XLA Modules:
  0.0 37.7 jit_solution(8623157536725170450)
XLA Ops:
  0.6 35.0 %shard_map.120 = (f32[640,512]{1,0:T(8,128)S(1)}, f32[640,512]{1,0:T(8,128)S(1)}, f32[16,512]{1,0:T(8,128)S(1)}, f32[16,128]{1,0:T(8,128)S(1)}, f32[16,128]{1,0:...) custom-call(s32[4]{0:T(128)} %lengths_ref.1, ...), custom_call_target="tpu_custom_call" | custom-call | tf_op jit(solution)/shard_map/pallas_call | solution.py:533
  35.6 2.1 %shard_map.121 = (f32[640,512]{1,0:T(8,128)}, f32[640,512]{1,0:T(8,128)}, bf16[4,4,512]{2,1,0:T(4,128)(2,1)}, bf16[4,4,1280]{2,1,0:T(4,128)(2,1)}) custom-call(f32[640,512]{1,0:T(8,128)S(1)} %get-tuple-element.13.one_ref, f32[640,512]{1,0:T(8,128)S(1)} %get-tuple-element.14.two_ref, f32[16,512]{1,0:T(8,128)S(1)} %get-tuple-element.15.proj_ref, ...), custom_call_target="tpu_custom_call" | custom-call | tf_op jit(solution)/shard_map/pallas_call | solution.py:581
